TPU v7x, 256 devices: a whole 4x4x8 slice. The times are simulated.
256 devices in a mesh: dp: 8 (over z), mp: 32 (over x, y, core).
Axes of the slice: x: 4, y: 4, z: 8, core: 2. Of those that a mesh axis runs over, the one named last changes fastest.
Arguments:
- activations: bfloat16 [12288, 8192], P('dp', 'mp'), may hold values from -6 to 6
- grad_output: bfloat16 [12288, 16384], P('dp', 'mp'), may hold values from -0.0546875 to 0.0546875
- holder_index: int32 [32, 32, 1], replicated, may hold values from 0 to 31; in each aligned block of 32 rows (0 to 31, 32 to 63, ..., all dimensions but the last counted through in order) no two rows name the same one
- row_offset: int32 [32, 32], replicated, may hold values from 0 to 1
- column_offset: int32 [32, 32], replicated, may hold values from 0 to 3
- live_counts: int32 [32], replicated, may hold values from 1 to 32, as said below
Outputs:
- candidate_grads: float32 [32, 32, 128, 128], P('mp', 'dp')
Inputs may be any that keep to these rules, and one draw needn't show every extreme that they name: In each owner's 32 slots at most 1 have the same holder_index, a bound that some block reaches. Slots from live_counts[o] on are unused; some owner uses all 32 slots.
All inputs are finite; a program needn't handle non-finite values.
Results may differ from a plain program's by a relative error of at most 0.0003.
Values may be sent and summed in bfloat16 or wider, within the bound.
A program may use at most 192 MiB of HBM per device.

v0:
```python
import jax
import jax.numpy as jnp
from jax import lax
from jax.sharding import PartitionSpec as P

BLK = 128


def on_device(activations, grad_output, holder_index, row_offset, column_offset, live_counts):
    owners = lax.axis_size("mp")
    my_index = lax.axis_index("mp")
    tokens_here = activations.shape[0]
    block_size = BLK
    per_holder = activations.shape[1] // block_size
    per_owner = grad_output.shape[1] // block_size
    slot_count = row_offset.shape[1]
    holders_all = holder_index[:, :, 0]
    my_holder = lax.dynamic_index_in_dim(holders_all, my_index, 0, keepdims=False)
    my_offset = lax.dynamic_index_in_dim(row_offset, my_index, 0, keepdims=False)
    my_column = lax.dynamic_index_in_dim(column_offset, my_index, 0, keepdims=False)
    my_count = lax.dynamic_index_in_dim(live_counts, my_index, 0, keepdims=False)
    grad_panels = grad_output.reshape(tokens_here, per_owner, block_size)
    is_used = jnp.arange(slot_count, dtype=jnp.int32) < my_count
    gathered = lax.all_gather(activations, "mp", axis=1, tiled=True)
    input_panels = gathered.reshape(tokens_here, owners * per_holder, block_size)
    picked_input = jnp.take(input_panels, my_holder * per_holder + my_offset, axis=1)
    picked_grad = jnp.take(grad_panels, my_column, axis=1)
    blocks = jnp.einsum(
        "tkr,tkc->krc", picked_input, picked_grad, preferred_element_type=jnp.float32
    )
    blocks = jnp.where(is_used[:, None, None], blocks, jnp.zeros_like(blocks))
    summed = lax.psum_scatter(blocks, "dp", scatter_dimension=0, tiled=True)
    return summed[None]


def solution(mesh):
    placed = (P("dp", "mp"), P("dp", "mp"), P(), P(), P(), P())
    return jax.shard_map(
        on_device, mesh=mesh, in_specs=placed, out_specs=P("mp", "dp", None, None), check_vma=False
    )
```

profile of v0, /device:TPU:8, one launch (start us, length us, event | category | flops | bytes accessed | tf_op | source)
XLA Modules:
  0.0 218.2 jit_solution(10876988246846555151)
XLA Ops:
  6.5 0.0 all-gather.2.cloned.1.call-start
  6.5 2.3 %copy.9 = bf16[1536,256]{0,1:T(8,128)(2,1)} copy(bf16[1536,256]{1,0:T(8,128)(2,1)} %param.6) | data formatting | bytes 1572864 | tf_op args[0]
  8.9 0.0 all-gather.2.cloned.1.call-update
  8.9 0.0 reduce-scatter.2.cloned.1.call-start
  9.0 1.7 copy.11
  10.7 0.9 copy.12
  11.6 1.2 dynamic_slice.14
  12.8 0.7 fusion.15
  13.5 6.5 %gather_fusion.1 = bf16[32,1536,128]{2,1,0:T(8,128)(2,1)} fusion(bf16[1536,4,128]{2,0,1:T(8,128)(2,1)S(1)} %copy.12, s32[1024]{0:T(1024)S(1)} %pad_clamp_fusion), kind=kCustom, calls=%fused_computation.1 | custom fusion | bytes 25165952 | tf_op jit(solution)/shard_map/jit(_take)/gather | solution.py:27
  20.1 0.6 iota_compare_fusion
  20.7 0.7 fusion.14
  21.4 0.7 compare_and_fusion
  22.1 86.9 %all-gather.2.cloned.1.call-done = bf16[1536,8192]{0,1:T(8,128)(2,1)} async-done(((bf16[1536,256]{0,1:T(8,128)(2,1)}), bf16[1536,8192]{0,1:T(8,128)(2,1)}) %all-gather.2.cloned.1.call-update) | async-done | bytes 25165840 | tf_op jit(solution)/shard_map/all_gather | solution.py:24
  109.1 32.4 %copy.10 = bf16[1536,64,128]{2,0,1:T(8,128)(2,1)} copy(bf16[1536,64,128]{0,2,1:T(8,128)(2,1)} %bitcast.34) | data formatting | bytes 50331648 | tf_op jit(solution)/shard_map/reshape | solution.py:25
  141.5 14.9 %gather_fusion = bf16[32,1536,128]{2,1,0:T(8,128)(2,1)} fusion(bf16[1536,64,128]{2,0,1:T(8,128)(2,1)} %copy.10, s32[1024]{0:T(1024)S(1)} %pad_clamp_fusion.1), kind=kCustom, calls=%fused_computation | custom fusion | bytes 25165952 | tf_op jit(solution)/shard_map/jit(_take)/gather | solution.py:26
  156.4 11.9 %fusion.8 = f32[32,128,128]{2,1,0:T(8,128)} fusion(bf16[32,1536,128]{2,1,0:T(8,128)(2,1)} %gather_fusion.1, pred[32]{0:T(512)(128)(4,1)S(1)} %get-tuple-element.5, bf16[32,1536,128]{2,1,0:T(8,128)(2,1)} %gather_fusion, pred[32]{0:T(512)(128)(4,1)S(1)} %get-tuple-element.6, pred[32]{0:T(512)(128)(4,1)S(1)} %iota_compare_fusion), kind=kOutput, calls=%fused_computation.10 | convolution fusion | flops 1623719936 | bytes 27263072 | tf_op jit(solution)/shard_map/tkr,tkc->krc/dot_general | solution.py:28
  168.4 0.0 reduce-scatter.2.cloned.1.call-update
  168.4 43.0 %reduce-scatter.2.cloned.1.call-done = f32[4,128,128]{2,1,0:T(8,128)} async-done(((f32[32,128,128]{2,1,0:T(8,128)}), f32[4,128,128]{2,1,0:T(8,128)}) %reduce-scatter.2.cloned.1.call-update) | async-done | bytes 262160 | tf_op jit(solution)/shard_map/reduce_scatter | solution.py:32
  (2 shorter events, 0.0 us)
Async XLA Ops:
  6.5 102.6 %all-gather.2.cloned.1.call-start = ((), (), s32[]{:S(2)}) async-start(), calls=%async_computation.1 | async-start | bytes 25952256 | tf_op jit(solution)/shard_map/all_gather | solution.py:24
  8.9 202.5 %reduce-scatter.2.cloned.1.call-start = ((), (), s32[]{:S(2)}) async-start(), calls=%async_computation.2 | async-start | bytes 2359296 | tf_op jit(solution)/shard_map/reduce_scatter | solution.py:32
Sparse Core Ops, SparseCore 0:
  9.9 99.1 all-gather.1
  168.5 42.8 reduce-scatter.1
where the time goes:
time: 219 us; the launch traced here: 218 us
  waiting for transfers between devices  130 us (59%)
  local copies, waits for them, and re-layouts  60.1 us (27%)
  between operations  13.4 us (6%)
  matrix products  11.9 us (5%)
  other arithmetic  2.77 us (1%)
    all_gather x1, waiting for transfers between devices, on_device(): gathered = lax.all_gather(activations, 'mp', axis=1, tiled=True)  86.9 us
    reduce_scatter x1, waiting for transfers between devices, on_device(): summed = lax.psum_scatter(blocks, 'dp', scatter_dimension=0, tiled=True)  43 us
    reshape x1, local copies, waits for them, and re-layouts, on_device(): gathered.reshape(tokens_here, owners * per_holder, block_size)  32.4 us
    gather x1, local copies, waits for them, and re-layouts, on_device(): jnp.take(input_panels, my_holder * per_holder + my_offset, axis=1)  14.9 us
    dot_general x1, matrix products, on_device(): jnp.einsum('tkr,tkc->krc', picked_input, picked_grad, preferred_element_t...  11.9 us
    gather x1, local copies, waits for them, and re-layouts, on_device(): picked_grad = jnp.take(grad_panels, my_column, axis=1)  6.53 us
  transfers between devices with their start and end apart: 2, of which 2 were waited for; matrix products, arithmetic and copies ran while one was open for 6% of the time, Pallas kernels for 0%

commit v1 on v0

v1 whole, which is shorter than its diff:
```python
import jax
import jax.numpy as jnp
from jax import lax
from jax.experimental import pallas as pl
from jax.experimental.pallas import tpu as pltpu
from jax.sharding import PartitionSpec as P

BLK = 128
SIDE = 4
RING = 8
CHUNKS = 6
MESH = pl.DeviceIdType.MESH
SIGNS = (1, -1)
PLACE = {0: 0, -1: 1, 1: 2, 2: 3}
LAST = CHUNKS - 1


def kernel(meta, a_hbm, g_hbm, out, *scratch):
    bufs = scratch[:CHUNKS]
    (acc, graw, gt, zrecv, a_sem, g_sem, p1_s, p1_r, q1_s, q1_r, p2_s, p2_r, q2_s, q2_r,
     sib_s, sib_r, z_s, z_r) = scratch[CHUNKS:]
    step = bufs[0].shape[1]
    me = lax.axis_index("mp")
    z = lax.axis_index("dp")
    core = me % 2
    y = (me // 2) % SIDE
    x = me // (2 * SIDE)

    def near(axis, sign):
        if axis == 0:
            there = (((x + sign + SIDE) % SIDE) * SIDE + y) * 2 + core
        else:
            there = (x * SIDE + (y + sign + SIDE) % SIDE) * 2 + core
        return {"mp": there}

    plane = {(axis, sign): near(axis, sign) for axis in (0, 1) for sign in SIGNS}
    sibling = {"mp": me + 1 - 2 * core}
    above = {sign: {"dp": (z + sign + RING) % RING} for sign in SIGNS}

    def remote(src, dst, send, recv, device):
        return pltpu.make_async_remote_copy(
            src_ref=src, dst_ref=dst, send_sem=send, recv_sem=recv, device_id=device, device_id_type=MESH
        )

    def at(half, rel, second, first, count=1):
        return pl.ds(((half * 2 + rel) * SIDE + second) * SIDE + first, count)

    def first_hop(c, h, sign):
        d = 0 if sign > 0 else 1
        return remote(bufs[c].at[at(h, 0, 0, 0)], bufs[c].at[at(h, 0, 0, PLACE[-sign])],
                      p1_s.at[c, h, d], p1_r.at[c, h, d], plane[h, sign])

    def first_relay(c, h):
        sign = 1 if (c + h) % 2 == 0 else -1
        return remote(bufs[c].at[at(h, 0, 0, PLACE[-sign])], bufs[c].at[at(h, 0, 0, 3)],
                      q1_s.at[c, h], q1_r.at[c, h], plane[h, sign])

    def row_hop(c, h, sign):
        d = 0 if sign > 0 else 1
        return remote(bufs[c].at[at(h, 0, 0, 0, 4)], bufs[c].at[at(h, 0, PLACE[-sign], 0, 4)],
                      p2_s.at[c, h, d], p2_r.at[c, h, d], plane[1 - h, sign])

    def row_relay(c, h, sign):
        d = 0 if sign > 0 else 1
        return remote(bufs[c].at[at(h, 0, PLACE[-sign], 2 * d, 2)], bufs[c].at[at(h, 0, 3, 2 * d, 2)],
                      q2_s.at[c, h, d], q2_r.at[c, h, d], plane[1 - h, sign])

    def share(c, h, piece):
        second, count = (0, 12) if piece == 0 else (3, 4)
        return remote(bufs[c].at[at(h, 0, second, 0, count)], bufs[c].at[at(h, 1, second, 0, count)],
                      sib_s.at[c, h, piece], sib_r.at[c, h, piece], sibling)

    def own(c, h):
        return pltpu.make_async_copy(
            a_hbm.at[pl.ds(c * step, step), pl.ds(h * BLK, BLK)],
            bufs[c].at[h * 32], a_sem.at[c, h])

    def panel(k):
        return pltpu.make_async_copy(g_hbm.at[:, pl.ds(k * BLK, BLK)], graw.at[k], g_sem.at[k])

    for c in range(CHUNKS):
        for h in (0, 1):
            own(c, h).start()
    for k in range(4):
        panel(k).start()

    barrier = pltpu.get_barrier_semaphore()
    peers = list(plane.values()) + [sibling] + list(above.values())
    for peer in peers:
        pl.semaphore_signal(barrier, inc=1, device_id=peer, device_id_type=MESH)
    pl.semaphore_wait(barrier, len(peers))

    for c in range(CHUNKS):
        for h in (0, 1):
            own(c, h).wait()
            for sign in SIGNS:
                first_hop(c, h, sign).start()

    for k in range(4):
        panel(k).wait()

    def turn(n, carry):
        for c in range(CHUNKS):
            gt[n, c] = graw[n, pl.ds(c * step, step), :].T
        return carry

    lax.fori_loop(0, 4, turn, 0)

    def products(c, g):
        base = ((z + g) % RING) * 4
        for i in range(4):
            word = meta[base + i]
            block = bufs[c][(word >> 2) & 63]
            part = jnp.dot(gt[word & 3, c], block, preferred_element_type=jnp.float32)
            if c == 0:
                acc[g, i] = part
            else:
                acc[g, i] += part

    def ring_size(sign, i):
        return 4 if (sign > 0) == (i < 2) else 3

    def z_hop(sign, i, t):
        d = 0 if sign > 0 else 1
        g = (sign * (ring_size(sign, i) - t)) % RING
        return g, remote(acc.at[g, i], zrecv.at[d, i, t], z_s.at[d, i, t], z_r.at[d, i, t], above[sign])

    long_chains = [(1, 0), (-1, 2), (1, 1), (-1, 3)]
    short_chains = [(1, 2), (-1, 0), (1, 3), (-1, 1)]

    for it in range(CHUNKS + 3):
        c = it
        if c < CHUNKS:
            for h in (0, 1):
                for sign in SIGNS:
                    first_hop(c, h, sign).wait_recv()
                first_relay(c, h).start()
            for h in (0, 1):
                first_relay(c, h).wait_recv()
                for sign in SIGNS:
                    row_hop(c, h, sign).start()
        c = it - 1
        if 0 <= c < CHUNKS:
            for h in (0, 1):
                for sign in SIGNS:
                    row_hop(c, h, sign).wait_recv()
                    row_relay(c, h, sign).start()
                share(c, h, 0).start()
        c = it - 2
        if 0 <= c < CHUNKS:
            for h in (0, 1):
                for sign in SIGNS:
                    row_relay(c, h, sign).wait_recv()
                share(c, h, 1).start()
        c = it - 3
        if 0 <= c < CHUNKS:
            for h in (0, 1):
                for piece in (0, 1):
                    share(c, h, piece).wait_recv()
            if c < LAST:
                def group(g, carry, c=c):
                    products(c, g)
                    return carry

                lax.fori_loop(0, RING, group, 0)

    products(LAST, 4)
    for sign, i in long_chains:
        z_hop(sign, i, 0)[1].start()

    def nearer(n, carry):
        products(LAST, 3 + 2 * n)
        return carry

    lax.fori_loop(0, 2, nearer, 0)
    for sign, i in short_chains:
        z_hop(sign, i, 0)[1].start()

    def rest(n, carry):
        products(LAST, (n + 6) % RING)
        return carry

    lax.fori_loop(0, 5, rest, 0)

    for t in range(1, 4):
        for sign, i in long_chains + (short_chains if t < 3 else []):
            d = 0 if sign > 0 else 1
            z_hop(sign, i, t - 1)[1].wait_recv()
            g, hop = z_hop(sign, i, t)
            acc[g, i] += zrecv[d, i, t - 1]
            hop.start()

    for c in range(CHUNKS):
        for h in (0, 1):
            for sign in SIGNS:
                first_hop(c, h, sign).wait_send()
                row_hop(c, h, sign).wait_send()
                row_relay(c, h, sign).wait_send()
            first_relay(c, h).wait_send()
            share(c, h, 0).wait_send()
            share(c, h, 1).wait_send()

    for i in (2, 0, 3, 1):
        total = acc[0, i]
        for sign in ((-1, 1) if i < 2 else (1, -1)):
            d = 0 if sign > 0 else 1
            t = ring_size(sign, i) - 1
            z_hop(sign, i, t)[1].wait_recv()
            total = total + zrecv[d, i, t]
        live = meta[z * 4 + i] >> 8
        out[i] = jnp.where(live > 0, total.T, jnp.zeros_like(total))

    for sign in SIGNS:
        for i in range(4):
            for t in range(ring_size(sign, i)):
                z_hop(sign, i, t)[1].wait_send()


def on_device(activations, grad_output, holder_index, row_offset, column_offset, live_counts):
    tokens, slots = activations.shape[0], row_offset.shape[1]
    step = tokens // CHUNKS
    me = lax.axis_index("mp")
    x, y, core = me >> 3, (me >> 1) & 3, me & 1
    holder = lax.dynamic_index_in_dim(holder_index[:, :, 0], me, 0, keepdims=False)
    half = lax.dynamic_index_in_dim(row_offset, me, 0, keepdims=False)
    column = lax.dynamic_index_in_dim(column_offset, me, 0, keepdims=False)
    count = lax.dynamic_index_in_dim(live_counts, me, 0, keepdims=False)

    def place(there, here):
        gap = (there - here) & 3
        return jnp.where(gap == 3, 1, jnp.where(gap == 0, 0, gap + 1))

    px, py = place(holder >> 3, x), place((holder >> 1) & 3, y)
    rel = (holder & 1) ^ core
    spot = half * 32 + rel * 16 + jnp.where(half == 0, py * 4 + px, px * 4 + py)
    used = (jnp.arange(slots, dtype=jnp.int32) < count).astype(jnp.int32)
    meta = spot * 4 + column + used * 256

    dma = pltpu.SemaphoreType.DMA
    out = pl.pallas_call(
        kernel,
        out_shape=jax.ShapeDtypeStruct((slots // RING, BLK, BLK), jnp.float32),
        in_specs=[
            pl.BlockSpec(memory_space=pltpu.SMEM),
            pl.BlockSpec(memory_space=pl.ANY),
            pl.BlockSpec(memory_space=pl.ANY),
        ],
        out_specs=pl.BlockSpec(memory_space=pltpu.VMEM),
        scratch_shapes=[pltpu.VMEM((64, step, BLK), jnp.bfloat16) for _ in range(CHUNKS)]
        + [
            pltpu.VMEM((RING, 4, BLK, BLK), jnp.float32),
            pltpu.VMEM((4, tokens, BLK), jnp.bfloat16),
            pltpu.VMEM((4, CHUNKS, BLK, step), jnp.bfloat16),
            pltpu.VMEM((2, 4, 4, BLK, BLK), jnp.float32),
            dma((CHUNKS, 2)),
            dma((4,)),
        ]
        + [dma((CHUNKS, 2, 2))] * 2
        + [dma((CHUNKS, 2))] * 2
        + [dma((CHUNKS, 2, 2))] * 6
        + [dma((2, 4, 4))] * 2,
        compiler_params=pltpu.CompilerParams(
            collective_id=0, has_side_effects=True, vmem_limit_bytes=56 * 1024 * 1024
        ),
    )(meta, activations, grad_output)
    return out[None]


def solution(mesh):
    placed = (P("dp", "mp"), P("dp", "mp"), P(), P(), P(), P())
    return jax.shard_map(
        on_device, mesh=mesh, in_specs=placed, out_specs=P("mp", "dp", None, None), check_vma=False
    )
```

time: 219 us -> 118 us (0.54)
  waiting for transfers between devices: 130 us -> 0 us
  Pallas kernels: 0 us -> 111 us
  local copies, waits for them, and re-layouts: 60.1 us -> 2.91 us
  between operations: 13.4 us -> 0.01 us
  matrix products: 11.9 us -> 0 us
    pallas_call x0 -> x1, Pallas kernels: none -> 111 us  [on_device(): pl.pallas_call(kernel, out_shape=jax.ShapeDtypeStruct((slots // RING, BLK...]
    all_gather x1 -> x0, waiting for transfers between devices: 86.9 us -> none  [on_device(): gathered = lax.all_gather(activations, 'mp', axis=1, tiled=True)]
    reduce_scatter x1 -> x0, waiting for transfers between devices: 43 us -> none  [on_device(): summed = lax.psum_scatter(blocks, 'dp', scatter_dimension=0, tiled=True)]
    reshape x2 -> x0, local copies, waits for them, and re-layouts: 33.3 us -> none  [the longest x1 32.4 us: on_device(): gathered.reshape(tokens_here, owners * per_holder, block_size)]
    gather x2 -> x0, local copies, waits for them, and re-layouts: 21.4 us -> none  [the longest x1 14.9 us: on_device(): jnp.take(input_panels, my_holder * per_holder + my_offset, axis=1)]
    dot_general x1 -> x0, matrix products: 11.9 us -> none  [on_device(): jnp.einsum('tkr,tkc->krc', picked_input, picked_grad, preferred_element_t...]
    unnamed x2 -> x1, local copies, waits for them, and re-layouts: 4.06 us -> 1.67 us
  transfers between devices with their start and end apart: 2 -> 0, of which waited for: 2 -> 0; matrix products, arithmetic and copies ran while one was open for 6% -> 0% of each run, Pallas kernels for 0% -> 0%
where the time goes in v1:
time: 118 us; the launch traced here: 116 us
  Pallas kernels  111 us (94%)
  local copies, waits for them, and re-layouts  2.91 us (2%)
  other arithmetic  1.95 us (2%)
    pallas_call x1, Pallas kernels, on_device(): pl.pallas_call(kernel, out_shape=jax.ShapeDtypeStruct((slots // RING, BLK...  111 us

profile of v1, /device:TPU:8, one launch (start us, length us, event | category | flops | bytes accessed | tf_op | source)
XLA Modules:
  0.0 116.0 jit_solution(9967416182443799762)
XLA Ops:
  0.0 1.2 %dynamic_slice.17 = s32[1]{0:T(128)} dynamic-slice(s32[32]{0:T(128)} %param.11, s32[]{:T(128)S(6)} %select_n.25), dynamic_slice_sizes={1} | dynamic-slice | bytes 12 | tf_op jit(solution)/shard_map/jit(dynamic_index_in_dim)/dynamic_slice | solution.py:227
  1.2 2.0 %fusion.2.meta = s32[32]{0:T(128)} fusion(s32[32,32]{1,0:T(8,128)} %param.10, s32[]{:T(128)S(6)} %select_n.25, s32[32,32,1]{1,2,0:T(1,128)} %param.8, s32[32,32]{1,0:T(8,128)} %param.9, s32[]{:T(128)} %bitcast.6, s32[]{:T(128)S(6)} %shift_right_arithmetic.17, s32[]{:T(128)S(6)} %and.28, s32[]{:T(128)S(6)} %and.26), kind=kLoop, calls=%fused_computation.11 | loop fusion | flops 1088 | bytes 532 | tf_op jit(solution)/shard_map/add | solution.py:237
  3.2 111.1 %shard_map.64 = f32[4,128,128]{2,1,0:T(8,128)} custom-call(s32[32]{0:T(128)} %fusion.2.meta, bf16[1536,256]{1,0:T(8,128)(2,1)} %a_hbm.1, bf16[1536,512]{1,0:T(8,128)(2,1)} %g_hbm.1), custom_call_target="tpu_custom_call" | custom-call | tf_op jit(solution)/shard_map/pallas_call | solution.py:240
  114.3 1.7 %copy.8 = f32[1,4,128,128]{3,2,1,0:T(8,128)} copy(f32[1,4,128,128]{3,2,1,0:T(8,128)} %bitcast.36) | data formatting | bytes 524288

commit v2 on v0

v2 whole, which is shorter than its diff:
```python
import jax
import jax.numpy as jnp
from jax import lax
from jax.experimental import pallas as pl
from jax.experimental.pallas import tpu as pltpu
from jax.sharding import PartitionSpec as P

BLK = 128
SIDE = 4
RING = 8
SIZES = (32, 32, 32, 32)
PIECES = len(SIZES)
STARTS = tuple(sum(SIZES[:p]) for p in range(PIECES))
LAG = 3
TURN = 256
MESH = pl.DeviceIdType.MESH
SIGNS = (1, -1)
PLACE = {0: 0, -1: 1, 1: 2, 2: 3}


def kernel(meta, a_hbm, g_hbm, out, *scratch):
    bufs = scratch[:PIECES]
    accs = scratch[PIECES : 2 * PIECES]
    lands = scratch[2 * PIECES : 3 * PIECES]
    (araw, graw, picked, a_sem, g_sem, p1_s, p1_r, q1_s, q1_r, p2_s, p2_r, q2_s, q2_r,
     sib_s, sib_r, z_s, z_r) = scratch[3 * PIECES :]
    me = lax.axis_index("mp")
    z = lax.axis_index("dp")
    core = me % 2
    y = (me // 2) % SIDE
    x = me // (2 * SIDE)

    def near(axis, sign):
        if axis == 0:
            there = (((x + sign + SIDE) % SIDE) * SIDE + y) * 2 + core
        else:
            there = (x * SIDE + (y + sign + SIDE) % SIDE) * 2 + core
        return {"mp": there}

    plane = {(axis, sign): near(axis, sign) for axis in (0, 1) for sign in SIGNS}
    sibling = {"mp": me + 1 - 2 * core}
    above = {sign: {"dp": (z + sign + RING) % RING} for sign in SIGNS}

    def remote(src, dst, send, recv, device):
        return pltpu.make_async_remote_copy(
            src_ref=src, dst_ref=dst, send_sem=send, recv_sem=recv, device_id=device, device_id_type=MESH
        )

    def at(half, rel, second, first, count=1):
        return pl.ds(((half * 2 + rel) * SIDE + second) * SIDE + first, count)

    def first_hop(p, h, sign):
        d = 0 if sign > 0 else 1
        return remote(bufs[p].at[at(h, 0, 0, 0)], bufs[p].at[at(h, 0, 0, PLACE[-sign])],
                      p1_s.at[p, h, d], p1_r.at[p, h, d], plane[h, sign])

    def first_relay(p, h):
        sign = 1 if (p + h) % 2 == 0 else -1
        return remote(bufs[p].at[at(h, 0, 0, PLACE[-sign])], bufs[p].at[at(h, 0, 0, 3)],
                      q1_s.at[p, h], q1_r.at[p, h], plane[h, sign])

    def row_hop(p, h, q, sign):
        d = 0 if sign > 0 else 1
        return remote(bufs[p].at[at(h, 0, 0, q)], bufs[p].at[at(h, 0, PLACE[-sign], q)],
                      p2_s.at[p, h, q, d], p2_r.at[p, h, q, d], plane[1 - h, sign])

    def row_relay(p, h, q):
        sign = 1 if q % 2 == 0 else -1
        return remote(bufs[p].at[at(h, 0, PLACE[-sign], q)], bufs[p].at[at(h, 0, 3, q)],
                      q2_s.at[p, h, q], q2_r.at[p, h, q], plane[1 - h, sign])

    def share(p, h, part):
        second, count = (0, 12) if part == 0 else (3, 4)
        return remote(bufs[p].at[at(h, 0, second, 0, count)], bufs[p].at[at(h, 1, second, 0, count)],
                      sib_s.at[p, h, part], sib_r.at[p, h, part], sibling)

    load = pltpu.make_async_copy(a_hbm, araw, a_sem)
    load.start()

    panels = pltpu.make_async_copy(g_hbm, graw, g_sem)
    panels.start()

    barrier = pltpu.get_barrier_semaphore()
    peers = list(plane.values()) + [sibling] + list(above.values())
    for peer in peers:
        pl.semaphore_signal(barrier, inc=1, device_id=peer, device_id_type=MESH)

    load.wait()
    for n in range(araw.shape[0] // TURN):
        for h in (0, 1):
            turned = araw[pl.ds(n * TURN, TURN), pl.ds(h * BLK, BLK)].T
            for p in range(PIECES):
                bufs[p][32 * h, :, pl.ds(n * TURN, TURN)] = turned[STARTS[p] : STARTS[p] + SIZES[p], :]

    pl.semaphore_wait(barrier, len(peers))

    for p in range(PIECES):
        for h in (0, 1):
            for sign in SIGNS:
                first_hop(p, h, sign).start()
    for p in range(PIECES):
        for h in (0, 1):
            for sign in SIGNS:
                first_hop(p, h, sign).wait_recv()
            first_relay(p, h).start()
    panels.wait()

    def products(p, n):
        size = SIZES[p]
        groups = (n + 4, 3 - n)
        words = [meta[me, ((z + g) % RING) * 4 + i] for g in groups for i in range(4)]
        for s, word in enumerate(words):
            picked[pl.ds(s * size, size), :] = bufs[p][(word >> 2) & 63]
        every = jnp.dot(picked[: 8 * size, :], graw[...], preferred_element_type=jnp.float32)
        for s, word in enumerate(words):
            part = every[s * size : (s + 1) * size]
            low = jnp.where((word & 1) == 0, part[:, :BLK], part[:, BLK : 2 * BLK])
            high = jnp.where((word & 1) == 0, part[:, 2 * BLK : 3 * BLK], part[:, 3 * BLK :])
            accs[p][groups[s // 4], s % 4] = jnp.where((word & 2) == 0, low, high)

    def hops(sign, u):
        return 4 if (sign > 0) == (u == 0) else 3

    def z_hop(p, sign, u, t):
        d = 0 if sign > 0 else 1
        g = (sign * (hops(sign, u) - t)) % RING
        return g, remote(accs[p].at[g, pl.ds(2 * u, 2)], lands[p].at[d, u, t],
                         z_s.at[p, d, u, t], z_r.at[p, d, u, t], above[sign])

    chains = [(1, 0), (-1, 1), (1, 1), (-1, 0)]

    def first_groups(p):
        for h in (0, 1):
            for part in (0, 1):
                share(p, h, part).wait_recv()

        def group(n, carry):
            products(p, n)
            return carry

        lax.fori_loop(0, 2, group, 0)
        for sign, u in chains:
            z_hop(p, sign, u, 0)[1].start()

    def other_groups(p):
        def group(n, carry):
            products(p, n)
            return carry

        lax.fori_loop(2, 4, group, 0)

    def z_step(p, t):
        for sign, u in chains:
            if t >= hops(sign, u):
                continue
            d = 0 if sign > 0 else 1
            z_hop(p, sign, u, t - 1)[1].wait_recv()
            g, hop = z_hop(p, sign, u, t)
            accs[p][g, pl.ds(2 * u, 2)] += lands[p][d, u, t - 1]
            hop.start()

    def z_end(p):
        for u in (1, 0):
            total = accs[p][0, pl.ds(2 * u, 2)]
            for sign in ((1, -1) if u else (-1, 1)):
                d = 0 if sign > 0 else 1
                t = hops(sign, u) - 1
                z_hop(p, sign, u, t)[1].wait_recv()
                total = total + lands[p][d, u, t]
            for i in (0, 1):
                live = meta[me, z * 4 + 2 * u + i] >> 8
                out[2 * u + i, pl.ds(STARTS[p], SIZES[p]), :] = jnp.where(
                    live > 0, total[i], jnp.zeros_like(total[i])
                )

    blocks = 4 * PIECES
    for k in range(blocks + LAG + 9):
        if k < blocks:
            p, q = k // 4, k % 4
            for h in (0, 1):
                if q == 3:
                    first_relay(p, h).wait_recv()
                for sign in SIGNS:
                    row_hop(p, h, q, sign).start()
        if 0 <= k - LAG < blocks:
            p, q = (k - LAG) // 4, (k - LAG) % 4
            for h in (0, 1):
                for sign in SIGNS:
                    row_hop(p, h, q, sign).wait_recv()
                row_relay(p, h, q).start()
            if q == 3:
                for h in (0, 1):
                    share(p, h, 0).start()
        for p in range(PIECES):
            since = k - (4 * p + 3 + LAG)
            if since == 2:
                for h in (0, 1):
                    for q in range(4):
                        row_relay(p, h, q).wait_recv()
                    share(p, h, 1).start()
            elif since == 3:
                first_groups(p)
            elif since == 4:
                other_groups(p)
            elif 5 <= since <= 7:
                z_step(p, since - 4)
            elif since == 8:
                z_end(p)

    for p in range(PIECES):
        for h in (0, 1):
            for sign in SIGNS:
                first_hop(p, h, sign).wait_send()
                for q in range(4):
                    row_hop(p, h, q, sign).wait_send()
            first_relay(p, h).wait_send()
            for q in range(4):
                row_relay(p, h, q).wait_send()
            for part in (0, 1):
                share(p, h, part).wait_send()
        for sign, u in chains:
            for t in range(hops(sign, u)):
                z_hop(p, sign, u, t)[1].wait_send()


def on_device(activations, grad_output, holder_index, row_offset, column_offset, live_counts):
    tokens, slots = activations.shape[0], row_offset.shape[1]
    mine = lax.broadcasted_iota(jnp.int32, row_offset.shape, 0)
    slot = lax.broadcasted_iota(jnp.int32, row_offset.shape, 1)
    holder = holder_index[:, :, 0]

    def place(gap):
        gap = gap & 3
        return jnp.where(gap == 3, 1, jnp.where(gap == 0, 0, gap + 1))

    px = place((holder >> 3) - (mine >> 3))
    py = place((holder >> 1) - (mine >> 1))
    rel = (holder ^ mine) & 1
    spot = row_offset * 32 + rel * 16 + jnp.where(row_offset == 0, py * 4 + px, px * 4 + py)
    used = (slot < live_counts[:, None]).astype(jnp.int32)
    meta = spot * 4 + column_offset + used * 256

    dma = pltpu.SemaphoreType.DMA
    out = pl.pallas_call(
        kernel,
        out_shape=jax.ShapeDtypeStruct((slots // RING, BLK, BLK), jnp.float32),
        in_specs=[
            pl.BlockSpec(memory_space=pltpu.SMEM),
            pl.BlockSpec(memory_space=pl.ANY),
            pl.BlockSpec(memory_space=pl.ANY),
        ],
        out_specs=pl.BlockSpec(memory_space=pltpu.VMEM),
        scratch_shapes=[pltpu.VMEM((64, size, tokens), jnp.bfloat16) for size in SIZES]
        + [pltpu.VMEM((RING, 4, size, BLK), jnp.float32) for size in SIZES]
        + [pltpu.VMEM((2, 2, 4, 2, size, BLK), jnp.float32) for size in SIZES]
        + [
            pltpu.VMEM(activations.shape, jnp.bfloat16),
            pltpu.VMEM(grad_output.shape, jnp.bfloat16),
            pltpu.VMEM((8 * max(SIZES), tokens), jnp.bfloat16),
            dma,
            dma,
        ]
        + [dma((PIECES, 2, 2))] * 2
        + [dma((PIECES, 2))] * 2
        + [dma((PIECES, 2, 4, 2))] * 2
        + [dma((PIECES, 2, 4))] * 2
        + [dma((PIECES, 2, 2))] * 2
        + [dma((PIECES, 2, 2, 4))] * 2,
        compiler_params=pltpu.CompilerParams(
            collective_id=0, has_side_effects=True, vmem_limit_bytes=56 * 1024 * 1024
        ),
    )(meta, activations, grad_output)
    return out[None]


def solution(mesh):
    placed = (P("dp", "mp"), P("dp", "mp"), P(), P(), P(), P())
    return jax.shard_map(
        on_device, mesh=mesh, in_specs=placed, out_specs=P("mp", "dp", None, None), check_vma=False
    )
```

time: 219 us -> 104 us (0.47)
  waiting for transfers between devices: 130 us -> 0 us
  Pallas kernels: 0 us -> 99.9 us
  local copies, waits for them, and re-layouts: 60.1 us -> 1.67 us
  between operations: 13.4 us -> 0.01 us
  matrix products: 11.9 us -> 0 us
    pallas_call x0 -> x1, Pallas kernels: none -> 99.9 us  [on_device(): pl.pallas_call(kernel, out_shape=jax.ShapeDtypeStruct((slots // RING, BLK...]
    all_gather x1 -> x0, waiting for transfers between devices: 86.9 us -> none  [on_device(): gathered = lax.all_gather(activations, 'mp', axis=1, tiled=True)]
    reduce_scatter x1 -> x0, waiting for transfers between devices: 43 us -> none  [on_device(): summed = lax.psum_scatter(blocks, 'dp', scatter_dimension=0, tiled=True)]
    reshape x2 -> x0, local copies, waits for them, and re-layouts: 33.3 us -> none  [the longest x1 32.4 us: on_device(): gathered.reshape(tokens_here, owners * per_holder, block_size)]
    gather x2 -> x0, local copies, waits for them, and re-layouts: 21.4 us -> none  [the longest x1 14.9 us: on_device(): jnp.take(input_panels, my_holder * per_holder + my_offset, axis=1)]
    dot_general x1 -> x0, matrix products: 11.9 us -> none  [on_device(): jnp.einsum('tkr,tkc->krc', picked_input, picked_grad, preferred_element_t...]
    unnamed x2 -> x1, local copies, waits for them, and re-layouts: 4.06 us -> 1.67 us
  transfers between devices with their start and end apart: 2 -> 0, of which waited for: 2 -> 0; matrix products, arithmetic and copies ran while one was open for 6% -> 0% of each run, Pallas kernels for 0% -> 0%
where the time goes in v2:
time: 104 us; the launch traced here: 103 us
  Pallas kernels  99.9 us (96%)
  local copies, waits for them, and re-layouts  1.67 us (2%)
  other arithmetic  1.45 us (1%)
    pallas_call x1, Pallas kernels, on_device(): pl.pallas_call(kernel, out_shape=jax.ShapeDtypeStruct((slots // RING, BLK...  99.9 us

profile of v2, /device:TPU:8, one launch (start us, length us, event | category | flops | bytes accessed | tf_op | source)
XLA Modules:
  0.0 103.0 jit_solution(9948056533282489137)
XLA Ops:
  0.0 1.4 %select_add_fusion.meta = s32[32,32]{1,0:T(8,128)} fusion(s32[32,32]{1,0:T(8,128)} %param.10, s32[32,32]{1,0:T(8,128)} %bitcast.3, s32[32,32]{1,0:T(8,128)} %param.9, s32[32]{0:T(128)} %param.11, s32[32]{0:T(128)S(1)} %get-tuple-element.5, s32[32]{0:T(128)S(1)} %get-tuple-element.6), kind=kLoop, calls=%fused_computation | loop fusion | flops 33792 | bytes 16768 | tf_op jit(solution)/shard_map/add | solution.py:241
  1.5 99.9 %shard_map.64 = f32[4,128,128]{2,1,0:T(8,128)} custom-call(s32[32,32]{1,0:T(8,128)} %select_add_fusion.meta, bf16[1536,256]{1,0:T(8,128)(2,1)} %a_hbm.1, bf16[1536,512]{1,0:T(8,128)(2,1)} %g_hbm.1), custom_call_target="tpu_custom_call" | custom-call | tf_op jit(solution)/shard_map/pallas_call | solution.py:244
  101.3 1.7 %copy.8 = f32[1,4,128,128]{3,2,1,0:T(8,128)} copy(f32[1,4,128,128]{3,2,1,0:T(8,128)} %bitcast.2) | data formatting | bytes 524288
  (1 shorter events, 0.0 us)

commit v3 on v2

v3 whole, which is shorter than its diff:
```python
import jax
import jax.numpy as jnp
from jax import lax
from jax.experimental import pallas as pl
from jax.experimental.pallas import tpu as pltpu
from jax.sharding import PartitionSpec as P

BLK = 128
SIDE = 4
RING = 8
SIZES = (48, 32, 32, 16)
PIECES = len(SIZES)
STARTS = tuple(sum(SIZES[:p]) for p in range(PIECES))
LAG = 96
TURN = 256
MESH = pl.DeviceIdType.MESH
SIGNS = (1, -1)
PLACE = {0: 0, -1: 1, 1: 2, 2: 3}


def kernel(holders, offsets, columns, counts, a_hbm, g_hbm, out, *scratch):
    bufs = scratch[:PIECES]
    accs = scratch[PIECES : 2 * PIECES]
    lands = scratch[2 * PIECES : 3 * PIECES]
    (holder_s, offset_s, column_s, count_s, meta, table_sem, araw, graw, picked, a_sem, g_sem, p1_s, p1_r, q1_s, q1_r, p2_s, p2_r, q2_s, q2_r,
     sib_s, sib_r, z_s, z_r) = scratch[3 * PIECES :]
    me = lax.axis_index("mp")
    z = lax.axis_index("dp")
    core = me % 2
    y = (me // 2) % SIDE
    x = me // (2 * SIDE)

    def near(axis, sign):
        if axis == 0:
            there = (((x + sign + SIDE) % SIDE) * SIDE + y) * 2 + core
        else:
            there = (x * SIDE + (y + sign + SIDE) % SIDE) * 2 + core
        return {"mp": there}

    plane = {(axis, sign): near(axis, sign) for axis in (0, 1) for sign in SIGNS}
    sibling = {"mp": me + 1 - 2 * core}
    above = {step: {"dp": (z + step + RING) % RING} for step in (1, -1, 2, -2)}

    def remote(src, dst, send, recv, device):
        return pltpu.make_async_remote_copy(
            src_ref=src, dst_ref=dst, send_sem=send, recv_sem=recv, device_id=device, device_id_type=MESH
        )

    def at(half, rel, second, first, count=1):
        return pl.ds(((half * 2 + rel) * SIDE + second) * SIDE + first, count)

    def first_hop(p, h, sign):
        d = 0 if sign > 0 else 1
        return remote(bufs[p].at[at(h, 0, 0, 0)], bufs[p].at[at(h, 0, 0, PLACE[-sign])],
                      p1_s.at[p, h, d], p1_r.at[p, h, d], plane[h, sign])

    def first_relay(p, h):
        sign = 1 if (p + h) % 2 == 0 else -1
        return remote(bufs[p].at[at(h, 0, 0, PLACE[-sign])], bufs[p].at[at(h, 0, 0, 3)],
                      q1_s.at[p, h], q1_r.at[p, h], plane[h, sign])

    def row_hop(p, h, q, sign):
        d = 0 if sign > 0 else 1
        return remote(bufs[p].at[at(h, 0, 0, q)], bufs[p].at[at(h, 0, PLACE[-sign], q)],
                      p2_s.at[p, h, q, d], p2_r.at[p, h, q, d], plane[1 - h, sign])

    def row_relay(p, h, q):
        sign = 1 if q % 2 == 0 else -1
        return remote(bufs[p].at[at(h, 0, PLACE[-sign], q)], bufs[p].at[at(h, 0, 3, q)],
                      q2_s.at[p, h, q], q2_r.at[p, h, q], plane[1 - h, sign])

    def share(p, h, part):
        second, count = (0, 12) if part == 0 else (3, 4)
        return remote(bufs[p].at[at(h, 0, second, 0, count)], bufs[p].at[at(h, 1, second, 0, count)],
                      sib_s.at[p, h, part], sib_r.at[p, h, part], sibling)

    load = pltpu.make_async_copy(a_hbm, araw, a_sem)
    load.start()

    panels = pltpu.make_async_copy(g_hbm, graw, g_sem)
    panels.start()
    tables = [
        pltpu.make_async_copy(src, dst, table_sem.at[n])
        for n, (src, dst) in enumerate(
            ((holders.at[me], holder_s), (offsets, offset_s), (columns, column_s), (counts, count_s))
        )
    ]
    for table in tables:
        table.start()

    barrier = pltpu.get_barrier_semaphore()
    peers = list(plane.values()) + [sibling] + list(above.values())
    for peer in peers:
        pl.semaphore_signal(barrier, inc=1, device_id=peer, device_id_type=MESH)

    load.wait()
    for n in range(araw.shape[0] // TURN):
        for h in (0, 1):
            turned = araw[pl.ds(n * TURN, TURN), pl.ds(h * BLK, BLK)].T
            for p in range(PIECES):
                bufs[p][32 * h, :, pl.ds(n * TURN, TURN)] = turned[STARTS[p] : STARTS[p] + SIZES[p], :]

    pl.semaphore_wait(barrier, len(peers))

    for p in range(PIECES):
        for h in (0, 1):
            for sign in SIGNS:
                first_hop(p, h, sign).start()
    for p in range(PIECES):
        for h in (0, 1):
            for sign in SIGNS:
                first_hop(p, h, sign).wait_recv()
            first_relay(p, h).start()
    panels.wait()
    for table in tables:
        table.wait()

    def place(gap):
        gap = gap & 3
        return jnp.where(gap == 3, 1, jnp.where(gap == 0, 0, gap + 1))

    def note(j, carry):
        holder, half = holder_s[0, j], offset_s[me, j]
        px, py = place((holder >> 3) - x), place(((holder >> 1) & 3) - y)
        spot = half * 32 + ((holder ^ core) & 1) * 16 + jnp.where(half == 0, py * 4 + px, px * 4 + py)
        meta[j] = spot * 4 + column_s[me, j] + jnp.where(j < count_s[me], 256, 0)
        return carry

    lax.fori_loop(0, 32, note, 0)

    def products(p, n):
        size = SIZES[p]
        groups = (n + 4, 3 - n)
        words = [meta[((z + g) % RING) * 4 + i] for g in groups for i in range(4)]
        for s, word in enumerate(words):
            picked[pl.ds(s * size, size), :] = bufs[p][(word >> 2) & 63]
        every = jnp.dot(picked[: 8 * size, :], graw[...], preferred_element_type=jnp.float32)
        for s, word in enumerate(words):
            part = every[s * size : (s + 1) * size]
            low = jnp.where((word & 1) == 0, part[:, :BLK], part[:, BLK : 2 * BLK])
            high = jnp.where((word & 1) == 0, part[:, 2 * BLK : 3 * BLK], part[:, 3 * BLK :])
            accs[p][groups[s // 4], s % 4] = jnp.where((word & 2) == 0, low, high)

    def leaf(p, name):
        acc, land = accs[p], lands[p]
        src, dst, step, n = {
            "far_up": (acc.at[4, pl.ds(0, 2)], land.at[0, pl.ds(0, 2)], 2, 0),
            "far_down": (acc.at[4, pl.ds(2, 2)], land.at[0, pl.ds(2, 2)], -2, 1),
            "third_up": (acc.at[3], land.at[1], 1, 2),
            "third_down": (acc.at[5], land.at[2], -1, 3),
            "next_up": (acc.at[1], land.at[3], 1, 4),
            "next_down": (acc.at[7], land.at[4], -1, 5),
            "sum_up": (acc.at[2], land.at[5], 2, 6),
            "sum_down": (acc.at[6], land.at[6], -2, 7),
        }[name]
        return remote(src, dst, z_s.at[p, n], z_r.at[p, n], above[step])

    names = ("far_up", "far_down", "third_up", "third_down", "next_up", "next_down", "sum_up", "sum_down")

    def ready(p):
        for h in (0, 1):
            for q in range(4):
                row_relay(p, h, q).wait_recv()
            share(p, h, 1).start()

    def first_groups(p):
        for h in (0, 1):
            for part in (0, 1):
                share(p, h, part).wait_recv()

        def group(n, carry):
            products(p, n)
            return carry

        lax.fori_loop(0, 2, group, 0)
        for name in names[:4]:
            leaf(p, name).start()

    def other_groups(p):
        def group(n, carry):
            products(p, n)
            return carry

        lax.fori_loop(2, 4, group, 0)
        for name in names[4:6]:
            leaf(p, name).start()

    def gather(p):
        acc, land = accs[p], lands[p]
        for name in names[:4]:
            leaf(p, name).wait_recv()
        acc[2] += land[1]
        acc[2, pl.ds(0, 2)] += land[0, pl.ds(0, 2)]
        acc[6] += land[2]
        acc[6, pl.ds(2, 2)] += land[0, pl.ds(2, 2)]
        leaf(p, "sum_up").start()
        leaf(p, "sum_down").start()

    def finish(p):
        for name in names[4:]:
            leaf(p, name).wait_recv()
        land = lands[p]
        total = accs[p][0] + ((land[3] + land[4]) + (land[5] + land[6]))
        for i in range(4):
            live = meta[z * 4 + i] >> 8
            out[i, pl.ds(STARTS[p], SIZES[p]), :] = jnp.where(live > 0, total[i], jnp.zeros_like(total[i]))

    order = [(p, q) for p in range(PIECES) for q in range(4)]
    stages = (ready, first_groups, other_groups, gather, finish)
    due = []
    for p in range(PIECES):
        after = SIZES[min(p + 1, PIECES - 1)]
        waits = (2, 3, 4, 6, 8) if after > 16 or p == PIECES - 1 else (3, 5, 6, 9, 11)
        due += [(4 * p + 3 + wait, p, stage) for wait, stage in zip(waits, stages)]
    due.sort(key=lambda entry: entry[:2])

    def sends(p, n):
        return {1: (0, 2, 1, 3)[n], -1: (1, 3, 0, 2)[n]} if p else {1: n, -1: n}

    def pass_on(k):
        p, n = order[k]
        for h in (0, 1):
            for sign, q in sends(p, n).items():
                row_hop(p, h, q, sign).wait_recv()
                if (q % 2 == 0) == (sign > 0):
                    row_relay(p, h, q).start()
        if n == 3:
            for h in (0, 1):
                share(p, h, 0).start()
        while due and due[0][0] <= k:
            _, p, stage = due.pop(0)
            stage(p)

    behind = passed = 0
    for p, n in order:
        for h in (0, 1):
            if n == (1 if p else 3):
                first_relay(p, h).wait_recv()
            for sign, q in sends(p, n).items():
                row_hop(p, h, q, sign).start()
        behind += SIZES[p]
        while behind - SIZES[order[passed][0]] >= LAG:
            behind -= SIZES[order[passed][0]]
            pass_on(passed)
            passed += 1
    for k in range(passed, len(order)):
        pass_on(k)

    def settle():
        for p in range(PIECES):
            for h in (0, 1):
                for sign in SIGNS:
                    first_hop(p, h, sign).wait_send()
                    for q in range(4):
                        row_hop(p, h, q, sign).wait_send()
                first_relay(p, h).wait_send()
                for q in range(4):
                    row_relay(p, h, q).wait_send()
                for part in (0, 1):
                    share(p, h, part).wait_send()

    for _, p, stage in due:
        stage(p)
        if p == PIECES - 1 and stage is other_groups:
            settle()
    for p in range(PIECES):
        for name in names:
            leaf(p, name).wait_send()


def on_device(activations, grad_output, holder_index, row_offset, column_offset, live_counts):
    tokens, slots = activations.shape[0], row_offset.shape[1]
    dma = pltpu.SemaphoreType.DMA
    out = pl.pallas_call(
        kernel,
        out_shape=pltpu.VMEM((slots // RING, BLK, BLK), jnp.float32),
        in_specs=[pl.BlockSpec(memory_space=pl.ANY)] * 6,
        out_specs=pl.BlockSpec(memory_space=pltpu.VMEM),
        scratch_shapes=[pltpu.VMEM((64, size, tokens), jnp.bfloat16) for size in SIZES]
        + [pltpu.VMEM((RING, 4, size, BLK), jnp.float32) for size in SIZES]
        + [pltpu.VMEM((7, 4, size, BLK), jnp.float32) for size in SIZES]
        + [
            pltpu.SMEM((1, slots), jnp.int32),
            pltpu.SMEM(row_offset.shape, jnp.int32),
            pltpu.SMEM(row_offset.shape, jnp.int32),
            pltpu.SMEM(live_counts.shape, jnp.int32),
            pltpu.SMEM((slots,), jnp.int32),
            dma((4,)),
            pltpu.VMEM(activations.shape, jnp.bfloat16),
            pltpu.VMEM(grad_output.shape, jnp.bfloat16),
            pltpu.VMEM((8 * max(SIZES), tokens), jnp.bfloat16),
            dma,
            dma,
        ]
        + [dma((PIECES, 2, 2))] * 2
        + [dma((PIECES, 2))] * 2
        + [dma((PIECES, 2, 4, 2))] * 2
        + [dma((PIECES, 2, 4))] * 2
        + [dma((PIECES, 2, 2))] * 2
        + [dma((PIECES, 8))] * 2,
        compiler_params=pltpu.CompilerParams(
            collective_id=0, has_side_effects=True, vmem_limit_bytes=56 * 1024 * 1024
        ),
    )(holder_index.transpose(0, 2, 1), row_offset, column_offset, live_counts, activations, grad_output)
    return out[None]


def solution(mesh):
    placed = (P("dp", "mp"), P("dp", "mp"), P(), P(), P(), P())
    return jax.shard_map(
        on_device, mesh=mesh, in_specs=placed, out_specs=P("mp", "dp", None, None), check_vma=False
    )
```

time: 104 us -> 93.3 us (0.90)
  Pallas kernels: 99.9 us -> 91.3 us
  other arithmetic: 1.45 us -> 0 us
    pallas_call x1, Pallas kernels: 99.9 us -> 91.3 us  [on_device(): pl.pallas_call(kernel, out_shape=pltpu.VMEM((slots // RING, BLK, BLK), jn...]
    add x1 -> x0, other arithmetic: 1.45 us -> none  [on_device(): meta = spot * 4 + column_offset + used * 256]
where the time goes in v3:
time: 93.3 us; the launch traced here: 92 us
  Pallas kernels  91.3 us (98%)
    pallas_call x1, Pallas kernels, on_device(): pl.pallas_call(kernel, out_shape=pltpu.VMEM((slots // RING, BLK, BLK), jn...  91.3 us

profile of v3, /device:TPU:8, one launch (start us, length us, event | category | flops | bytes accessed | tf_op | source)
XLA Modules:
  0.0 92.0 jit_solution(3000570618764530387)
XLA Ops:
  0.0 91.3 %shard_map.64 = f32[4,128,128]{2,1,0:T(8,128)S(1)} custom-call(s32[32,1,32]{2,1,0:T(1,128)} %bitcast.3, s32[32,32]{1,0:T(8,128)} %offsets.1, s32[32,32]{1,0:T(8,128)} %columns.1, s32[32]{0:T(128)} %counts.1, bf16[1536,256]{1,0:T(8,128)(2,1)} %a_hbm.1, bf16[1536,512]{1,0:T(8,128)(2,1)} %g_hbm.1), custom_call_target="tpu_custom_call" | custom-call | tf_op jit(solution)/shard_map/pallas_call | solution.py:274
  91.3 0.7 copy.8

commit v4 on v3

--- a/solution.py
+++ b/solution.py
@@ -210,7 +210,11 @@
     due = []
     for p in range(PIECES):
         after = SIZES[min(p + 1, PIECES - 1)]
-        waits = (2, 3, 4, 6, 8) if after > 16 or p == PIECES - 1 else (3, 5, 6, 9, 11)
+        waits = (2, 3, 4, 6, 8)
+        if p < PIECES - 1:
+            waits = (2, 4, 5, 8, 10) if after == 16 else (1, 2, 3, 5, 7)
+        if p == 0:
+            waits = (1, 2, 3, 5, 7)
         due += [(4 * p + 3 + wait, p, stage) for wait, stage in zip(waits, stages)]
     due.sort(key=lambda entry: entry[:2])
 

time: 93.3 us -> 92.9 us (level)
  no operation moved by 1% of the time
where the time goes in v4:
time: 92.9 us; the launch traced here: 92.1 us
  Pallas kernels  91.4 us (98%)
    pallas_call x1, Pallas kernels, on_device(): pl.pallas_call(kernel, out_shape=pltpu.VMEM((slots // RING, BLK, BLK), jn...  91.4 us

profile of v4, /device:TPU:8, one launch (start us, length us, event | category | flops | bytes accessed | tf_op | source)
XLA Modules:
  0.0 92.1 jit_solution(8136946022046303145)
XLA Ops:
  0.0 91.4 %shard_map.64 = f32[4,128,128]{2,1,0:T(8,128)S(1)} custom-call(s32[32,1,32]{2,1,0:T(1,128)} %bitcast.3, s32[32,32]{1,0:T(8,128)} %offsets.1, s32[32,32]{1,0:T(8,128)} %columns.1, s32[32]{0:T(128)} %counts.1, bf16[1536,256]{1,0:T(8,128)(2,1)} %a_hbm.1, bf16[1536,512]{1,0:T(8,128)(2,1)} %g_hbm.1), custom_call_target="tpu_custom_call" | custom-call | tf_op jit(solution)/shard_map/pallas_call | solution.py:278
  91.4 0.7 copy.8
